TPU v7x, 32 devices: a whole 2x2x4 slice. The times are simulated.
32 devices in a mesh: gx: 8 (over z, y), gy: 4 (over x, core).
Axes of the slice: x: 2, y: 2, z: 4, core: 2. Of those that a mesh axis runs over, the one named last changes fastest.
Arguments:
- forces: float32 [3, 128, 128, 256], P(None, 'gx', 'gy'), may hold values from -8 to 8
- pressure_prev: float32 [128, 128, 256], P('gx', 'gy'), may hold values from -8 to 8
Outputs:
- pressure: float32 [128, 128, 256], P('gx', 'gy')
- residual: float32 [128, 128, 256], P('gx', 'gy')
All inputs are finite; a program needn't handle non-finite values.
Results may differ from a plain program's by a relative error of at most 0.0003.
Values sent between devices are 32-bit elements; how exact they have to be, the bound alone decides.
A program may use at most 64 MiB of HBM per device.

v0:
```python
import jax
import jax.numpy as jnp
from jax import lax
from jax.sharding import PartitionSpec as P

LEVELS = 5
SWEEPS = 2
COARSE_SWEEPS = 4
CYCLES = 2


OMEGA = 0.8


def padded_2(x, sides, width):
    for axis, dim in sides:
        peers, length = (lax.axis_size(axis), x.shape[dim])
        up = [(i, (i + 1) % peers) for i in range(peers)]
        down = [(j, i) for i, j in up]
        last = lax.slice_in_dim(x, length - width, length, axis=dim)
        initial = lax.slice_in_dim(x, 0, width, axis=dim)
        before = lax.ppermute(last, axis, up)
        after = lax.ppermute(initial, axis, down)
        x = jnp.concatenate([before, x, after], axis=dim)
    return x


def shifted(block, axis, distance):
    devices = range(lax.axis_size(axis))
    route = [((i - distance) % len(devices), i) for i in devices]
    return lax.ppermute(block, axis, route)


def vertical(values):
    padded = jnp.pad(values, ((0, 0), (0, 0), (1, 1)))
    return padded[:, :, 2:] + padded[:, :, :-2]


def operate_padded(padded, weight):
    center = padded[1:-1, 1:-1]
    beside = padded[2:, 1:-1] + padded[:-2, 1:-1] + padded[1:-1, 2:] + padded[1:-1, :-2]
    return weight * (4.0 * center - beside) + (2.0 * center - vertical(center))


def relax(padded, source, weight):
    center = padded[1:-1, 1:-1]
    return center + OMEGA * (source - operate_padded(padded, weight)) / (4.0 * weight + 2.0)


def wrapped(values):
    return jnp.pad(values, ((1, 1), (1, 1), (0, 0)), mode="wrap")


def restrict(residual_now):
    rows_x, rows_y, depth = residual_now.shape
    return 0.25 * residual_now.reshape(rows_x // 2, 2, rows_y // 2, 2, depth).sum(axis=(1, 3))


def prolong(correction):
    return jnp.repeat(jnp.repeat(correction, 2, axis=0), 2, axis=1)


def mean_mode(values, source):
    depth = source.shape[2]
    column = jnp.mean(source, axis=(0, 1))
    lower = jnp.concatenate([jnp.zeros((1,), source.dtype), -jnp.ones((depth - 1,), source.dtype)])
    upper = jnp.concatenate([-jnp.ones((depth - 1,), source.dtype), jnp.zeros((1,), source.dtype)])
    middle = 2.0 * jnp.ones((depth,), source.dtype)
    profile = lax.linalg.tridiagonal_solve(lower, middle, upper, column[:, None])[:, 0]
    return values + profile[None, None, :]


def whole_cycle(values, source, level_index):
    weight = 0.25**level_index
    if level_index == LEVELS - 1:
        values = mean_mode(values, source)
        for sweep_index in range(COARSE_SWEEPS):
            values = relax(wrapped(values), source, weight)
        return values
    for sweep_index in range(SWEEPS):
        values = relax(wrapped(values), source, weight)
    residual_now = source - operate_padded(wrapped(values), weight)
    coarse_source = restrict(residual_now)
    correction = whole_cycle(jnp.zeros_like(coarse_source), coarse_source, level_index + 1)
    values = values + prolong(correction)
    for sweep_index in range(SWEEPS):
        values = relax(wrapped(values), source, weight)
    return values


def rimmed(values):
    return padded_2(values, (("gx", 0), ("gy", 1)), 1)


def smooth_local(values, source, weight):
    for sweep_index in range(SWEEPS):
        values = relax(rimmed(values), source, weight)
    return values


def local_cycle(values, source, level_index, gather_level):
    weight = 0.25**level_index
    if level_index == gather_level:
        gathered = lax.all_gather(source, "gy", axis=1, tiled=True)
        gathered = lax.all_gather(gathered, "gx", axis=0, tiled=True)
        solved = whole_cycle(jnp.zeros_like(gathered), gathered, level_index)
        start_x = lax.axis_index("gx") * source.shape[0]
        start_y = lax.axis_index("gy") * source.shape[1]
        return lax.dynamic_slice(solved, (start_x, start_y, jnp.int32(0)), source.shape)
    values = smooth_local(values, source, weight)
    residual_now = source - operate_padded(rimmed(values), weight)
    coarse_source = restrict(residual_now)
    correction = local_cycle(
        jnp.zeros_like(coarse_source), coarse_source, level_index + 1, gather_level
    )
    values = values + prolong(correction)
    return smooth_local(values, source, weight)


def on_device(forces, pressure_prev):
    force_x, force_y, force_z = (forces[0], forces[1], forces[2])
    from_left = shifted(force_x[-1:], "gx", 1)
    from_below = shifted(force_y[:, -1:], "gy", 1)
    behind_x = jnp.concatenate([from_left, force_x[:-1]], axis=0)
    behind_y = jnp.concatenate([from_below, force_y[:, :-1]], axis=1)
    behind_z = jnp.pad(force_z[:, :, :-1], ((0, 0), (0, 0), (1, 0)))
    source = behind_x - force_x + (behind_y - force_y) + (behind_z - force_z)
    gather_level = LEVELS - 2
    pressure = pressure_prev
    for cycle_index in range(CYCLES):
        pressure = local_cycle(pressure, source, 0, gather_level)
    residual = source - operate_padded(rimmed(pressure), 1.0)
    return (pressure, residual)


def solution(mesh):
    return jax.shard_map(
        on_device,
        mesh=mesh,
        in_specs=(P(None, "gx", "gy", None), P("gx", "gy", None)),
        out_specs=(P("gx", "gy", None), P("gx", "gy", None)),
        check_vma=False,
    )
```

profile of v0, /device:TPU:13, one launch (start us, length us, event | category | flops | bytes accessed | tf_op | source)
XLA Modules:
  0.0 1442.6 jit_solution(10738329578411890575)
XLA Ops:
  35.9 2.7 collective-permute-start.18
  46.0 4.3 collective-permute-start.22
  60.5 2.7 collective-permute-start.30
  70.4 4.2 collective-permute-start.34
  82.0 5.9 all_gather.12
  87.8 23.4 %all_gather.13 = f32[16,16,256]{2,1,0:T(8,128)S(1)} all-gather(f32[2,16,256]{2,1,0:T(8,128)S(1)} %copy.7), channel_id=1, replica_groups=mesh['gx'=8,'gy'=4] {'gx'}, dimensions={0}, use_global_device_ids=true | all-gather | bytes 294912 | tf_op jit(solution)/shard_map/all_gather | solution.py:105
  114.7 172.0 %while.64 = (s32[]{:T(128)}, f32[]{:T(128)}, f32[1]{0:T(128)}, f32[7,32]{1,0:T(8,128)S(1)}, f32[7,32,1]{1,2,0:T(1,128)S(1)}, /*index=5*/f32[7,32,1]{1,2,0:T(1,12...) while((s32[]{:T(128)}, f32[]{:T(128)}, f32[1]{0:T(128)}, f32[7,32]{1,0:T(8,128)S(1)}, ...), condition=%wide.region_6.7_spmd, body=%wide.region_5.6_spmd.sunk | while | flops 194 | bytes 4729 | solution.py:69
  312.2 300.4 %while.65 = (s32[]{:T(128)}, f32[1]{0:T(128)}, f32[7,32,1]{1,2,0:T(1,128)S(1)}, f32[7,32,1]{1,2,0:T(1,128)S(1)}, f32[7,32]{1,0:T(8,128)S(1)}, /*index=5*/s32[]{:T(128)}, s32[]{:T(128)}) while((s32[]{:T(128)}, f32[1]{0:T(128)}, f32[7,32,1]{1,2,0:T(1,128)S(1)}, f32[7,32,1]{1,2,0:T(1,128)S(1)}, f32[7,32]{1,0:T(8,128)S(1)}, /*index=5*/s32[]{:T(128)}, ...), condition=%wide.region_8.9_spmd, body=%wide.region_7.8_spmd.sunk | while | flops 67 | bytes 3173 | solution.py:69
  652.8 3.9 collective-permute-start.38
  659.2 8.0 collective-permute-start.40
  679.4 2.7 collective-permute-start.46
  689.5 2.5 collective-permute-start.50
  700.2 2.5 collective-permute-start.54
  711.0 2.5 collective-permute-start.58
  721.2 2.5 collective-permute-start.62
  731.7 2.5 collective-permute-start.66
  742.2 2.5 collective-permute-start.70
  793.4 5.9 all_gather.14
  799.3 22.9 %all_gather.15 = f32[16,16,256]{2,1,0:T(8,128)S(1)} all-gather(f32[2,16,256]{2,1,0:T(8,128)S(1)} %copy.9), channel_id=1, replica_groups=mesh['gx'=8,'gy'=4] {'gx'}, dimensions={0}, use_global_device_ids=true | all-gather | bytes 294912 | tf_op jit(solution)/shard_map/all_gather | solution.py:105
  825.7 170.6 %while.66 = (s32[]{:T(128)}, f32[]{:T(128)}, f32[1]{0:T(128)}, f32[7,32]{1,0:T(8,128)S(1)}, f32[7,32,1]{1,2,0:T(1,128)S(1)}, /*index=5*/f32[7,32,1]{1,2,0:T(1,12...) while((s32[]{:T(128)}, f32[]{:T(128)}, f32[1]{0:T(128)}, ...), condition=%wide.region_15.16_spmd, body=%wide.region_14.15_spmd.sunk | while | flops 194 | bytes 4729 | solution.py:69
  1021.8 300.7 %while.67 = (s32[]{:T(128)}, f32[1]{0:T(128)}, f32[7,32,1]{1,2,0:T(1,128)S(1)}, f32[7,32,1]{1,2,0:T(1,128)S(1)}, f32[7,32]{1,0:T(8,128)S(1)}, /*index=5*/s32[]{:T(128)}, s32[]{:T(128)}) while((s32[]{:T(128)}, f32[1]{0:T(128)}, f32[7,32,1]{1,2,0:T(1,128)S(1)}, f32[7,32,1]{1,2,0:T(1,128)S(1)}, f32[7,32]{1,0:T(8,128)S(1)}, ...), condition=%wide.region_17.18_spmd, body=%wide.region_16.17_spmd.sunk | while | flops 67 | bytes 3173 | solution.py:69
  1362.7 3.9 collective-permute-start.90
  1369.1 8.0 collective-permute-start.92
  1389.3 2.7 collective-permute-start.98
  (679 shorter events, 325.8 us)
Async XLA Ops:
  1.6 7.3 collective-permute-start.3
  2.8 6.2 collective-permute-start.2
  4.4 6.5 collective-permute-start.1
  21.8 5.1 collective-permute-start.10
  24.6 5.3 collective-permute-start.14
  25.9 5.9 collective-permute-start.15
  27.2 7.2 collective-permute-start.12
  29.0 5.5 collective-permute-start.13
  46.0 6.7 collective-permute-start.22
  50.4 6.0 collective-permute-start.26
  53.2 5.9 collective-permute-start.24
  70.4 5.0 collective-permute-start.34
  652.8 4.7 collective-permute-start.38
  659.2 10.3 collective-permute-start.40
  705.6 4.9 collective-permute-start.56
  726.6 4.6 collective-permute-start.64
  737.2 4.6 collective-permute-start.68
  747.9 4.6 collective-permute-start.72
  1362.7 4.7 collective-permute-start.90
  1369.1 10.2 collective-permute-start.92
  1404.9 4.6 collective-permute-start.104
  1415.8 4.6 collective-permute-start.108
  1426.3 4.6 collective-permute-start.112
  1436.8 4.6 collective-permute-start.116
  (97 other events, 325.6 us)
where the time goes:
time: 1460 us; the launch traced here: 1440 us
  loops' own time  877 us (60%)
  starting transfers between devices  185 us (13%)
  between operations  124 us (8%)
  waiting for transfers between devices  102 us (7%)
  local copies, waits for them, and re-layouts  83.8 us (6%)
  blocking collectives  58.2 us (4%)
    another operation x4, loops' own time, mean_mode(): lax.linalg.tridiagonal_solve(lower, middle, upper, column[:, None])[:, 0]  877 us
    ppermute x58, starting transfers between devices, padded_2(): after = lax.ppermute(initial, axis, down)  143 us
    slice x102, local copies, waits for them, and re-layouts, mean_mode(): lax.linalg.tridiagonal_solve(lower, middle, upper, column[:, None])[:, 0]  69.6 us
    ppermute x58, waiting for transfers between devices, padded_2(): after = lax.ppermute(initial, axis, down)  58.8 us
    all_gather x2, blocking collectives, local_cycle(): gathered = lax.all_gather(gathered, 'gx', axis=0, tiled=True)  46.4 us
    ppermute x58, waiting for transfers between devices, padded_2(): before = lax.ppermute(last, axis, up)  43.2 us
    ppermute x58, starting transfers between devices, padded_2(): before = lax.ppermute(last, axis, up)  36.6 us
  transfers between devices with their start and end apart: 118, of which 77 were waited for; matrix products, arithmetic and copies ran while one was open for 0% of the time, Pallas kernels for 0%

commit v1 on v0

v1 whole, which is shorter than its diff:
```python
import functools

import jax
import jax.numpy as jnp
from jax import lax
from jax.experimental import pallas as pl
from jax.experimental.pallas import tpu as pltpu
from jax.sharding import PartitionSpec as P

OMEGA = 0.8
PAD = 8
DIRS = [(dx, dy) for dx in (-1, 0, 1) for dy in (-1, 0, 1) if (dx, dy) != (0, 0)]
MESH = pl.DeviceIdType.MESH


def loop(count, body):
    def step(i, carry):
        body(i)
        return carry

    lax.fori_loop(0, count, step, 0)


def vertical(c):
    depth = c.shape[-1]
    axis = c.ndim - 1
    lane = lax.broadcasted_iota(jnp.int32, c.shape, axis)
    below = jnp.where(lane == 0, 0.0, pltpu.roll(c, 1, axis))
    above = jnp.where(lane == depth - 1, 0.0, pltpu.roll(c, depth - 1, axis))
    return below + above


def parts(ref, row, count):
    block = ref[pl.ds(row - 1, count + 2)]
    c = block[1:-1]
    width = c.shape[1]
    lateral = (block[:-2] + block[2:]) + (pltpu.roll(c, 1, 1) + pltpu.roll(c, width - 1, 1))
    return c, lateral, vertical(c)


def sweep(src, f, dst, row, rows, weight, unit, cols=None):
    k = OMEGA / (4.0 * weight + 2.0)

    def body(i):
        r = row + i * unit
        c, lateral, up = parts(src, r, unit)
        new = (1.0 - OMEGA) * c + k * (weight * lateral + up + f[pl.ds(r, unit)])
        if cols is None:
            dst[pl.ds(r, unit)] = new
        else:
            dst[pl.ds(r, unit), cols[0] : cols[1]] = new[:, cols[0] : cols[1]]

    loop(rows // unit, body)


def sweep_twice_from_zero(f, dst, row, rows, weight, unit):
    k = OMEGA / (4.0 * weight + 2.0)

    def body(i):
        r = row + i * unit
        c, lateral, up = parts(f, r, unit)
        dst[pl.ds(r, unit)] = k * ((2.0 - OMEGA) * c + k * (weight * lateral + up))

    loop(rows // unit, body)


def residual_rows(v, f, r, count, weight):
    c, lateral, up = parts(v, r, count)
    return f[pl.ds(r, count)] - ((4.0 * weight + 2.0) * c - weight * lateral - up)


def restricted(v, f, tmp, row, rows, cols, weight, put):
    start, count = cols
    depth = v.shape[-1]

    def body(i):
        r = residual_rows(v, f, row + 2 * i, 2, weight)
        both = r[0] + r[1]
        width = both.shape[0]
        halves = []
        for h in range(depth // 128):
            tmp[h, 0:width] = both[:, h * 128 : (h + 1) * 128]
            halves.append(
                tmp[h, pl.ds(start, count // 2, 2)] + tmp[h, pl.ds(start + 1, count // 2, 2)]
            )
        put(i, 0.25 * jnp.concatenate(halves, axis=1))

    loop(rows // 2, body)


def doubled(e, tmp, start):
    width, depth = e.shape
    for h in range(depth // 128):
        piece = e[:, h * 128 : (h + 1) * 128]
        tmp[h, pl.ds(start, width, 2)] = piece
        tmp[h, pl.ds(start + 1, width, 2)] = piece


def read_tmp(tmp, start, width):
    return jnp.concatenate([tmp[h, pl.ds(start, width)] for h in range(tmp.shape[0])], axis=1)


def ghosts(v, rows):
    v[0] = v[rows]
    v[rows + 1] = v[1]


def kernel(
    nx, ny, cycles,
    forces, pressure, out_p, out_r,
    fx, fy, fz, s, pa, pb, t0, t1, res,
    f1a, f1b, v1a, v1b, f2a, f2b, v2a, v2b, f3, v3a, v3b, f4, v4a, v4b, green, tmp,
    local_sem, plane_send, plane_recv, halo_send, halo_recv,
    g_send, g_recv, h_send, h_recv,
):
    mx, my = lax.axis_index("gx"), lax.axis_index("gy")
    n = nx * ny
    me = mx * ny + my
    bx, by, depth = pressure.shape
    cx1, cy1 = bx // 2, by // 2
    cx2, cy2 = bx // 4, by // 4

    loads = [
        pltpu.make_async_copy(forces.at[0], fx.at[pl.ds(1, bx)], local_sem.at[0]),
        pltpu.make_async_copy(forces.at[1], fy.at[:, pl.ds(PAD, by)], local_sem.at[1]),
        pltpu.make_async_copy(pressure, pa.at[pl.ds(PAD, bx), pl.ds(PAD, by)], local_sem.at[2]),
        pltpu.make_async_copy(forces.at[2], fz, local_sem.at[3]),
    ]
    for load in loads:
        load.start()

    barrier = pltpu.get_barrier_semaphore()

    def greet(j):
        other = lax.rem(me + 1 + j, n)
        pl.semaphore_signal(barrier, inc=1, device_id=(other // ny, lax.rem(other, ny)), device_id_type=MESH)

    loop(n - 1, greet)

    row_i = lax.broadcasted_iota(jnp.int32, (depth, depth), 0).astype(jnp.float32)
    col_i = lax.broadcasted_iota(jnp.int32, (depth, depth), 1).astype(jnp.float32)
    green[...] = (jnp.minimum(row_i, col_i) + 1.0) * (depth - jnp.maximum(row_i, col_i)) / (depth + 1.0)

    pl.semaphore_wait(barrier, n - 1)

    sends = []

    def halo(ref, size, width, slot):
        sx, sy = size
        copies = []
        for d, (dx, dy) in sorted(enumerate(DIRS), key=lambda e: abs(e[1][0]) * abs(e[1][1])):
            w = width - 1 if dx and dy else width
            if dx == 0:
                src_r, dst_r = pl.ds(PAD, sx), pl.ds(PAD, sx)
            elif dx == 1:
                src_r, dst_r = pl.ds(PAD + sx - w, w), pl.ds(PAD - w, w)
            else:
                src_r, dst_r = pl.ds(PAD, w), pl.ds(PAD + sx, w)
            if dy == 0:
                src_c, dst_c = pl.ds(PAD, sy), pl.ds(PAD, sy)
            elif dy == 1:
                src_c, dst_c = pl.ds(sy, PAD), pl.ds(0, PAD)
            else:
                src_c, dst_c = pl.ds(PAD, PAD), pl.ds(PAD + sy, PAD)
            copy = pltpu.make_async_remote_copy(
                src_ref=ref.at[src_r, src_c],
                dst_ref=ref.at[dst_r, dst_c],
                send_sem=halo_send.at[slot, d],
                recv_sem=halo_recv.at[slot, d],
                device_id=(lax.rem(mx + dx + nx, nx), lax.rem(my + dy + ny, ny)),
                device_id_type=MESH,
            )
            copy.start()
            copies.append(copy)
        sends.extend(copies)
        return copies

    def arrive(copies):
        for copy in copies:
            copy.wait_recv()

    right, above = lax.rem(mx + 1, nx), lax.rem(my + 1, ny)
    loads[0].wait()
    plane_x = pltpu.make_async_remote_copy(
        src_ref=fx.at[pl.ds(bx, 1)], dst_ref=fx.at[pl.ds(0, 1)],
        send_sem=plane_send.at[0], recv_sem=plane_recv.at[0],
        device_id=(right, my), device_id_type=MESH,
    )
    plane_x.start()
    loads[1].wait()
    plane_y = pltpu.make_async_remote_copy(
        src_ref=fy.at[:, pl.ds(by, PAD)], dst_ref=fy.at[:, pl.ds(0, PAD)],
        send_sem=plane_send.at[1], recv_sem=plane_recv.at[1],
        device_id=(mx, above), device_id_type=MESH,
    )
    plane_y.start()
    sends.extend([plane_x, plane_y])
    loads[2].wait()
    coming_p = halo(pa, (bx, by), 4, 0)
    loads[3].wait()
    plane_x.wait_recv()
    plane_y.wait_recv()

    def make_source(i):
        r = 2 * i
        x = fx[pl.ds(r, 3)]
        y = fy[pl.ds(r, 2)]
        z = fz[pl.ds(r, 2)]
        lane = lax.broadcasted_iota(jnp.int32, z.shape, 2)
        behind_z = jnp.where(lane == 0, 0.0, pltpu.roll(z, 1, 2))
        behind_y = pltpu.roll(y, 1, 1)[:, PAD:]
        s[pl.ds(PAD + r, 2), PAD : PAD + by] = (
            (x[:-1] - x[1:]) + (behind_y - y[:, PAD:]) + (behind_z - z)
        )

    loop(bx // 2, make_source)
    coming_s = halo(s, (bx, by), 4, 1)
    arrive(coming_p)
    arrive(coming_s)

    half = ny // 2
    many = nx * half
    parity = lax.rem(my, 2)
    partner = my + 1 - 2 * parity
    mine = mx * half + my // 2

    def solve_2(f2, turn):
        def place(x, y):
            return f2.at[pl.ds(1 + x * cx2, cx2), pl.ds(pl.multiple_of(y * cy2, cy2), cy2)]

        def direct(x, y, ident, to):
            return pltpu.make_async_remote_copy(
                src_ref=place(x, y), dst_ref=place(x, y),
                send_sem=g_send.at[turn, to], recv_sem=g_recv.at[turn, ident],
                device_id=(to // half, 2 * lax.rem(to, half) + parity), device_id_type=MESH,
            )

        def onward(x, y, ident):
            return pltpu.make_async_remote_copy(
                src_ref=place(x, y), dst_ref=place(x, y),
                send_sem=h_send.at[turn, ident], recv_sem=h_recv.at[turn, ident],
                device_id=(mx, partner), device_id_type=MESH,
            )

        def spot(ident, par):
            return ident // half, 2 * lax.rem(ident, half) + par

        def start(j):
            direct(mx, my, mine, lax.rem(mine + 1 + j, many)).start()

        loop(many - 1, start)
        onward(mx, my, mine).start()

        def pass_on(j):
            ident = lax.rem(mine + many - 1 - j, many)
            x, y = spot(ident, parity)
            direct(x, y, ident, ident).wait_recv()
            onward(x, y, ident).start()

        loop(many - 1, pass_on)

        def other(ident):
            x, y = spot(ident, 1 - parity)
            onward(x, y, ident).wait_recv()

        loop(many, other)

        def finish():
            def done(j):
                ident = lax.rem(mine + 1 + j, many)
                direct(mx, my, mine, ident).wait_send()
                x, y = spot(ident, parity)
                onward(x, y, ident).wait_send()

            loop(many - 1, done)
            onward(mx, my, mine).wait_send()

        sizes = [(cx2 * nx, cy2 * ny)]
        for _ in range(2):
            sizes.append((sizes[-1][0] // 2, sizes[-1][1] // 2))
        (x2, y2), (x3, y3), (x4, y4) = sizes

        ghosts(f2, x2)
        sweep_twice_from_zero(f2, v2a, 1, x2, 0.25**2, 4)
        ghosts(v2a, x2)

        def put3(i, value):
            f3[1 + i] = value

        restricted(v2a, f2, tmp, 1, x2, (0, y2), 0.25**2, put3)
        ghosts(f3, x3)
        sweep_twice_from_zero(f3, v3a, 1, x3, 0.25**3, 4)
        ghosts(v3a, x3)

        def put4(i, value):
            f4[1 + i] = value

        restricted(v3a, f3, tmp, 1, x3, (0, y3), 0.25**3, put4)
        total = jnp.sum(jnp.sum(f4[pl.ds(1, x4)], axis=0), axis=0, keepdims=True) / (x4 * y4)
        u = jnp.dot(
            jnp.broadcast_to(total, (8, depth)), green[...],
            preferred_element_type=jnp.float32, precision=lax.Precision.HIGHEST,
        )
        v4a[...] = jnp.broadcast_to(u[0:1][None], v4a.shape)
        for src, dst in ((v4a, v4b), (v4b, v4a), (v4a, v4b), (v4b, v4a)):
            sweep(src, f4, dst, 1, x4, 0.25**4, 8)
            ghosts(dst, x4)

        def climb(e, v, rows, width):
            def body(i):
                doubled(e[1 + i], tmp, 0)
                v[pl.ds(1 + 2 * i, 2)] += read_tmp(tmp, 0, 2 * width)[None]

            loop(rows, body)
            ghosts(v, 2 * rows)

        climb(v4a, v3a, x4, y4)
        sweep(v3a, f3, v3b, 1, x3, 0.25**3, 4)
        ghosts(v3b, x3)
        sweep(v3b, f3, v3a, 1, x3, 0.25**3, 4)
        climb(v3a, v2a, x3, y3)
        sweep(v2a, f2, v2b, 1, x2, 0.25**2, 4)
        ghosts(v2b, x2)
        sweep(v2b, f2, v2a, 1, x2, 0.25**2, 4)
        return finish

    ends = []
    for turn in range(cycles):
        last = turn == cycles - 1
        w = 5 if last else 4
        p_in, f1, f2 = (pa, f1a, f2a) if turn % 2 == 0 else (pb, f1b, f2b)
        sweep(p_in, s, t0, PAD - (w - 1), bx + 2 * (w - 1), 1.0, 2)
        sweep(t0, s, t1, PAD - (w - 2), bx + 2 * (w - 2), 1.0, 2)

        def put1(i, value):
            f1[PAD + i, PAD : PAD + cy1] = value

        restricted(t1, s, tmp, PAD, bx, (PAD, by), 1.0, put1)
        arrive(halo(f1, (cx1, cy1), 5, 2 + 2 * turn))
        sweep_twice_from_zero(f1, v1a, PAD - 4, cx1 + 8, 0.25, 2)

        def put2(i, value):
            f2[1 + mx * cx2 + i, pl.ds(pl.multiple_of(my * cy2, cy2), cy2)] = value

        restricted(v1a, f1, tmp, PAD, cx1, (PAD, cy1), 0.25, put2)
        ends.append(solve_2(f2, turn))

        x2, y2 = cx2 * nx, cy2 * ny

        def down_to_1(i):
            q = lax.rem(mx * cx2 + i - 2 + x2, x2)
            doubled(v2a[1 + q], tmp, PAD)
            for h in range(tmp.shape[0]):
                tmp[h, 0:PAD] = tmp[h, 2 * y2 : 2 * y2 + PAD]
                tmp[h, 2 * y2 + PAD : 2 * y2 + 2 * PAD] = tmp[h, PAD : 2 * PAD]
            e = read_tmp(tmp, pl.multiple_of(my * cy1, PAD), cy1 + 2 * PAD)
            v1a[pl.ds(PAD - 4 + 2 * i, 2)] += e[None]

        loop(cx2 + 4, down_to_1)
        sweep(v1a, f1, v1b, PAD - 3, cx1 + 6, 0.25, 2)
        sweep(v1b, f1, v1a, PAD - 2, cx1 + 4, 0.25, 2)

        reach = 2 if last else 1

        def down_to_0(i):
            doubled(v1a[PAD - reach + i], tmp, 0)
            t1[pl.ds(PAD - 2 * reach + 2 * i, 2)] += read_tmp(tmp, PAD, by + 2 * PAD)[None]

        loop(cx1 + 2 * reach, down_to_0)
        sweep(t1, s, t0, PAD - (w - 3), bx + 2 * (w - 3), 1.0, 2)
        if last:
            sweep(t0, s, t1, PAD - 1, bx + 2, 1.0, 2)
        else:
            following = pb if turn % 2 == 0 else pa
            sweep(t0, s, following, PAD, bx, 1.0, 2, (PAD, PAD + by))
            arrive(halo(following, (bx, by), 5, 3 + 2 * turn))

    store_p = pltpu.make_async_copy(t1.at[pl.ds(PAD, bx), pl.ds(PAD, by)], out_p, local_sem.at[0])
    store_p.start()

    def last_residual(i):
        r = residual_rows(t1, s, PAD + 2 * i, 2, 1.0)
        res[pl.ds(2 * i, 2)] = r[:, PAD : PAD + by]

    loop(bx // 2, last_residual)
    store_r = pltpu.make_async_copy(res, out_r, local_sem.at[1])
    store_r.start()
    for copy in sends:
        copy.wait_send()
    for end in ends:
        end()
    store_p.wait()
    store_r.wait()


def on_device(nx, ny, forces, pressure_prev):
    bx, by, depth = pressure_prev.shape
    cycles = 2
    n = nx * ny
    f32 = jnp.float32

    def vmem(*shape):
        return pltpu.VMEM(shape + (depth,), f32)

    p0 = (bx + 2 * PAD, by + 2 * PAD)
    p1 = (bx // 2 + 2 * PAD, by // 2 + 2 * PAD)
    p2, p3, p4 = ((nx * bx // k + 2, ny * by // k) for k in (4, 8, 16))
    many = n // 2
    sem = pltpu.SemaphoreType.DMA
    scratch = (
        [vmem(bx + 1, by), vmem(bx, by + PAD), vmem(bx, by)]
        + [vmem(*p0)] * 5
        + [vmem(bx, by)]
        + [vmem(*p1)] * 4
        + [vmem(*p2)] * 4
        + [vmem(*p3)] * 3
        + [vmem(*p4)] * 3
        + [vmem(depth)]
        + [pltpu.VMEM((depth // 128, max(2 * p2[1], 2 * p1[1]) + 2 * PAD, 128), f32)]
        + [sem((4,)), sem((2,)), sem((2,))]
        + [sem((2 + 2 * cycles, 8))] * 2
        + [sem((cycles, many))] * 4
    )
    shape = jax.ShapeDtypeStruct((bx, by, depth), f32)
    anyspace = pl.BlockSpec(memory_space=pl.ANY)
    return pl.pallas_call(
        functools.partial(kernel, nx, ny, cycles),
        out_shape=(shape, shape),
        in_specs=[anyspace] * 2,
        out_specs=(anyspace, anyspace),
        scratch_shapes=scratch,
        compiler_params=pltpu.CompilerParams(
            collective_id=0, has_side_effects=True, vmem_limit_bytes=48 * 1024 * 1024
        ),
    )(forces, pressure_prev)


def solution(mesh):
    return jax.shard_map(
        functools.partial(on_device, mesh.shape["gx"], mesh.shape["gy"]),
        mesh=mesh,
        in_specs=(P(None, "gx", "gy", None), P("gx", "gy", None)),
        out_specs=(P("gx", "gy", None), P("gx", "gy", None)),
        check_vma=False,
    )
```

time: 1460 us -> 125 us (0.09); the launches traced: 1440 us -> 124 us
  loops' own time: 877 us -> 0 us
  starting transfers between devices: 185 us -> 0 us
  between operations: 124 us -> 0.65 us
  Pallas kernels: 0 us -> 120 us
  waiting for transfers between devices: 102 us -> 0 us
  local copies, waits for them, and re-layouts: 83.8 us -> 4.03 us
  blocking collectives: 58.2 us -> 0 us
    another operation x4 -> x0, loops' own time: 877 us -> none  [mean_mode(): lax.linalg.tridiagonal_solve(lower, middle, upper, column[:, None])[:, 0]]
    ppermute x118 -> x0, starting transfers between devices: 185 us -> none  [the longest x58 143 us: padded_2(): after = lax.ppermute(initial, axis, down)]
    pallas_call x0 -> x1, Pallas kernels: none -> 120 us  [on_device(): pl.pallas_call(functools.partial(kernel, nx, ny, cycles), out_shape=(shap...]
    ppermute x118 -> x0, waiting for transfers between devices: 102 us -> none  [the longest x58 58.8 us: padded_2(): after = lax.ppermute(initial, axis, down)]
    slice x149 -> x0, local copies, waits for them, and re-layouts: 70.8 us -> none  [the longest x102 69.6 us: mean_mode(): lax.linalg.tridiagonal_solve(lower, middle, upper, column[:, None])[:, 0]]
    all_gather x4 -> x0, blocking collectives: 58.2 us -> none  [the longest x2 46.4 us: local_cycle(): gathered = lax.all_gather(gathered, 'gx', axis=0, tiled=True)]
  transfers between devices with their start and end apart: 118 -> 0, of which waited for: 77 -> 0; matrix products, arithmetic and copies ran while one was open for 0% -> 0% of each run, Pallas kernels for 0% -> 0%
where the time goes in v1:
time: 125 us; the launch traced here: 124 us
  Pallas kernels  120 us (96%)
  local copies, waits for them, and re-layouts  4.03 us (3%)
    pallas_call x1, Pallas kernels, on_device(): pl.pallas_call(functools.partial(kernel, nx, ny, cycles), out_shape=(shap...  120 us
    unnamed x6, local copies, waits for them, and re-layouts  4.03 us

profile of v1, /device:TPU:13, one launch (start us, length us, event | category | flops | bytes accessed | tf_op | source)
XLA Modules:
  0.0 124.4 jit_solution(13560289383358518763)
XLA Ops:
  0.6 0.0 copy-start
  0.6 1.4 %copy-done = f32[3,16,32,256]{3,2,1,0:T(8,128)S(1)} copy-done((f32[3,16,32,256]{3,2,1,0:T(8,128)S(1)}, f32[3,16,32,256]{3,2,1,0:T(8,128)}, u32[]{:S(2)}) %copy-start) | copy-done | bytes 1572888
  2.0 0.0 copy-start.1
  2.0 1.0 copy-done.1
  3.1 119.7 %shard_map.41 = (f32[16,32,256]{2,1,0:T(8,128)S(1)}, f32[16,32,256]{2,1,0:T(8,128)S(1)}) custom-call(f32[3,16,32,256]{3,2,1,0:T(8,128)S(1)} %copy-done, f32[16,32,256]{2,1,0:T(8,128)S(1)} %copy-done.1), custom_call_target="tpu_custom_call" | custom-call | tf_op jit(solution)/shard_map/pallas_call | solution.py:426
  122.8 0.8 copy.6
  123.6 0.8 copy.7
Async XLA Ops:
  0.6 1.4 %copy-start = (f32[3,16,32,256]{3,2,1,0:T(8,128)S(1)}, f32[3,16,32,256]{3,2,1,0:T(8,128)}, u32[]{:S(2)}) copy-start(f32[3,16,32,256]{3,2,1,0:T(8,128)} %forces.1) | copy-start | bytes 4718596
  2.0 1.0 copy-start.1

commit v2 on v1

--- a/solution.py
+++ b/solution.py
@@ -9,7 +9,6 @@
 
 OMEGA = 0.8
 PAD = 8
-DIRS = [(dx, dy) for dx in (-1, 0, 1) for dy in (-1, 0, 1) if (dx, dy) != (0, 0)]
 MESH = pl.DeviceIdType.MESH
 
 
@@ -147,33 +146,47 @@
 
     def halo(ref, size, width, slot):
         sx, sy = size
-        copies = []
-        for d, (dx, dy) in sorted(enumerate(DIRS), key=lambda e: abs(e[1][0]) * abs(e[1][1])):
-            w = width - 1 if dx and dy else width
-            if dx == 0:
-                src_r, dst_r = pl.ds(PAD, sx), pl.ds(PAD, sx)
-            elif dx == 1:
-                src_r, dst_r = pl.ds(PAD + sx - w, w), pl.ds(PAD - w, w)
-            else:
-                src_r, dst_r = pl.ds(PAD, w), pl.ds(PAD + sx, w)
-            if dy == 0:
-                src_c, dst_c = pl.ds(PAD, sy), pl.ds(PAD, sy)
-            elif dy == 1:
-                src_c, dst_c = pl.ds(sy, PAD), pl.ds(0, PAD)
-            else:
-                src_c, dst_c = pl.ds(PAD, PAD), pl.ds(PAD + sy, PAD)
+        k = min(width, PAD)
+
+        def strip(d, rows, cols, step):
+            dx, dy = step
             copy = pltpu.make_async_remote_copy(
-                src_ref=ref.at[src_r, src_c],
-                dst_ref=ref.at[dst_r, dst_c],
+                src_ref=ref.at[rows[0], cols[0]],
+                dst_ref=ref.at[rows[1], cols[1]],
                 send_sem=halo_send.at[slot, d],
                 recv_sem=halo_recv.at[slot, d],
                 device_id=(lax.rem(mx + dx + nx, nx), lax.rem(my + dy + ny, ny)),
                 device_id_type=MESH,
             )
             copy.start()
-            copies.append(copy)
-        sends.extend(copies)
-        return copies
+            sends.append(copy)
+            return copy
+
+        def rows_for(dx, w):
+            if dx == 1:
+                return pl.ds(PAD + sx - w, w), pl.ds(PAD - w, w)
+            return pl.ds(PAD, w), pl.ds(PAD + sx, w)
+
+        rows = (pl.ds(PAD, sx), pl.ds(PAD, sx))
+        cols = (pl.ds(PAD, sy), pl.ds(PAD, sy))
+        low, high = pl.ds(PAD - k, k), pl.ds(PAD + sy, k)
+        beside = [
+            strip(0, rows, (pl.ds(PAD + sy - k, k), low), (0, 1)),
+            strip(1, rows, (pl.ds(PAD, k), high), (0, -1)),
+        ]
+        late = [
+            strip(2, rows_for(1, width), cols, (1, 0)),
+            strip(3, rows_for(-1, width), cols, (-1, 0)),
+        ]
+
+        def corners():
+            for copy in beside:
+                copy.wait_recv()
+            for d, (dx, side) in enumerate(((1, low), (1, high), (-1, low), (-1, high))):
+                late.append(strip(4 + d, rows_for(dx, width - 1), (side, side), (dx, 0)))
+            return late
+
+        return corners
 
     def arrive(copies):
         for copy in copies:
@@ -189,7 +202,7 @@
     plane_x.start()
     loads[1].wait()
     plane_y = pltpu.make_async_remote_copy(
-        src_ref=fy.at[:, pl.ds(by, PAD)], dst_ref=fy.at[:, pl.ds(0, PAD)],
+        src_ref=fy.at[:, pl.ds(PAD + by - 1, 1)], dst_ref=fy.at[:, pl.ds(PAD - 1, 1)],
         send_sem=plane_send.at[1], recv_sem=plane_recv.at[1],
         device_id=(mx, above), device_id_type=MESH,
     )
@@ -215,8 +228,7 @@
 
     loop(bx // 2, make_source)
     coming_s = halo(s, (bx, by), 4, 1)
-    arrive(coming_p)
-    arrive(coming_s)
+    coming = coming_p() + coming_s()
 
     half = ny // 2
     many = nx * half
@@ -289,7 +301,7 @@
 
         restricted(v2a, f2, tmp, 1, x2, (0, y2), 0.25**2, put3)
         ghosts(f3, x3)
-        sweep_twice_from_zero(f3, v3a, 1, x3, 0.25**3, 4)
+        sweep_twice_from_zero(f3, v3a, 1, x3, 0.25**3, 8)
         ghosts(v3a, x3)
 
         def put4(i, value):
@@ -315,9 +327,9 @@
             ghosts(v, 2 * rows)
 
         climb(v4a, v3a, x4, y4)
-        sweep(v3a, f3, v3b, 1, x3, 0.25**3, 4)
+        sweep(v3a, f3, v3b, 1, x3, 0.25**3, 8)
         ghosts(v3b, x3)
-        sweep(v3b, f3, v3a, 1, x3, 0.25**3, 4)
+        sweep(v3b, f3, v3a, 1, x3, 0.25**3, 8)
         climb(v3a, v2a, x3, y3)
         sweep(v2a, f2, v2b, 1, x2, 0.25**2, 4)
         ghosts(v2b, x2)
@@ -329,15 +341,23 @@
         last = turn == cycles - 1
         w = 5 if last else 4
         p_in, f1, f2 = (pa, f1a, f2a) if turn % 2 == 0 else (pb, f1b, f2b)
-        sweep(p_in, s, t0, PAD - (w - 1), bx + 2 * (w - 1), 1.0, 2)
-        sweep(t0, s, t1, PAD - (w - 2), bx + 2 * (w - 2), 1.0, 2)
+        inner = 1 + w % 2
+        sweep(p_in, s, t0, PAD + inner, bx - 2 * inner, 1.0, 2)
+        sweep(t0, s, t1, PAD + inner + 1, bx - 2 * inner - 2, 1.0, 2)
+        arrive(coming)
+        for src, dst, reach, off in ((p_in, t0, w - 1, inner), (t0, t1, w - 2, inner + 1)):
+            sweep(src, s, dst, PAD - reach, reach + off, 1.0, 2)
+            sweep(src, s, dst, PAD + bx - off, reach + off, 1.0, 2)
 
         def put1(i, value):
             f1[PAD + i, PAD : PAD + cy1] = value
 
         restricted(t1, s, tmp, PAD, bx, (PAD, by), 1.0, put1)
-        arrive(halo(f1, (cx1, cy1), 5, 2 + 2 * turn))
-        sweep_twice_from_zero(f1, v1a, PAD - 4, cx1 + 8, 0.25, 2)
+        coming = halo(f1, (cx1, cy1), 5, 2 + 2 * turn)()
+        sweep_twice_from_zero(f1, v1a, PAD + 2, cx1 - 4, 0.25, 2)
+        arrive(coming)
+        sweep_twice_from_zero(f1, v1a, PAD - 4, 6, 0.25, 2)
+        sweep_twice_from_zero(f1, v1a, PAD + cx1 - 2, 6, 0.25, 2)
 
         def put2(i, value):
             f2[1 + mx * cx2 + i, pl.ds(pl.multiple_of(my * cy2, cy2), cy2)] = value
@@ -373,7 +393,7 @@
         else:
             following = pb if turn % 2 == 0 else pa
             sweep(t0, s, following, PAD, bx, 1.0, 2, (PAD, PAD + by))
-            arrive(halo(following, (bx, by), 5, 3 + 2 * turn))
+            coming = halo(following, (bx, by), 5, 3 + 2 * turn)()
 
     store_p = pltpu.make_async_copy(t1.at[pl.ds(PAD, bx), pl.ds(PAD, by)], out_p, local_sem.at[0])
     store_p.start()

time: 125 us -> 113 us (0.904)
  Pallas kernels: 120 us -> 108 us
    pallas_call x1, Pallas kernels: 120 us -> 108 us  [on_device(): pl.pallas_call(functools.partial(kernel, nx, ny, cycles), out_shape=(shap...]
where the time goes in v2:
time: 113 us
  Pallas kernels  108 us (96%)
  local copies, waits for them, and re-layouts  4.03 us (4%)
    pallas_call x1, Pallas kernels, on_device(): pl.pallas_call(functools.partial(kernel, nx, ny, cycles), out_shape=(shap...  108 us
    unnamed x6, local copies, waits for them, and re-layouts  4.03 us

profile of v2, /device:TPU:13, one launch (start us, length us, event | category | flops | bytes accessed | tf_op | source)
XLA Modules:
  0.0 113.1 jit_solution(7913451618883445042)
XLA Ops:
  0.6 0.0 copy-start
  0.6 1.4 %copy-done = f32[3,16,32,256]{3,2,1,0:T(8,128)S(1)} copy-done((f32[3,16,32,256]{3,2,1,0:T(8,128)S(1)}, f32[3,16,32,256]{3,2,1,0:T(8,128)}, u32[]{:S(2)}) %copy-start) | copy-done | bytes 1572888
  2.0 0.0 copy-start.1
  2.0 1.0 copy-done.1
  3.1 108.4 %shard_map.41 = (f32[16,32,256]{2,1,0:T(8,128)S(1)}, f32[16,32,256]{2,1,0:T(8,128)S(1)}) custom-call(f32[3,16,32,256]{3,2,1,0:T(8,128)S(1)} %copy-done, f32[16,32,256]{2,1,0:T(8,128)S(1)} %copy-done.1), custom_call_target="tpu_custom_call" | custom-call | tf_op jit(solution)/shard_map/pallas_call | solution.py:446
  111.5 0.8 copy.6
  112.3 0.8 copy.7
Async XLA Ops:
  0.6 1.4 %copy-start = (f32[3,16,32,256]{3,2,1,0:T(8,128)S(1)}, f32[3,16,32,256]{3,2,1,0:T(8,128)}, u32[]{:S(2)}) copy-start(f32[3,16,32,256]{3,2,1,0:T(8,128)} %forces.1) | copy-start | bytes 4718596
  2.0 1.0 copy-start.1
